TPU v7x, 128 devices: a whole 4x4x4 slice. The times are simulated.
128 devices in a mesh: narrow: 2 (over core), wide: 64 (over x, y, z).
Axes of the slice: x: 4, y: 4, z: 4, core: 2. Of those that a mesh axis runs over, the one named last changes fastest.
Arguments:
- embeddings: bfloat16 [32768, 256], P(('narrow', 'wide')), may hold values from -6 to 6
- noise: float32 [32768], P(('narrow', 'wide')), may hold values from 0.05 to 0.5
- targets: float32 [32768, 64], P(('narrow', 'wide')), may hold values from -6 to 6
- level_scale: float32 [7], replicated, may hold values from 1.5 to 4
- skeleton: int32 [7, 128, 256], P(None, ('narrow', 'wide')), may hold values from 0 to 32767, as said below
Outputs:
- solution: float32 [32768, 64], P(('narrow', 'wide'))
- fit: float32 [64], replicated
- logdet: float32 [], replicated
Inputs may be any that keep to these rules, and one draw needn't show every extreme that they name: `skeleton`: for each level l (first index l - 1), all devices whose index in narrow+wide has the same quotient by 2**l hold equal rows, and each row holds 256 distinct indices of points of that level-l node.
All inputs are finite; a program needn't handle non-finite values.
Results may differ from a plain program's by a relative error of at most 0.0003.
Values may be sent and summed in bfloat16 or wider, within the bound.
A program may use at most 128 MiB of HBM per device.

v0:
```python
import functools

import jax
import jax.numpy as jnp
from jax import lax
from jax.experimental import pallas as pl
from jax.experimental.pallas import tpu as pltpu
from jax.sharding import PartitionSpec as P

NARROW_WIDE = ("narrow", "wide")
MESH = pl.DeviceIdType.MESH
EXACT = lax.Precision.HIGHEST
CLOSE = lax.Precision.HIGH
LANES = 128
VMEM = pltpu.VMEM


def exact_dot(left, right):
    return jnp.dot(left, right, precision=EXACT, preferred_element_type=jnp.float32)


def unit(k):
    return jnp.where(lax.broadcasted_iota(jnp.int32, (8, LANES), 0) == k, 1.0, 0.0)


def inverse8(cols):
    cols = list(cols)
    logs = jnp.zeros((1, LANES), jnp.float32)
    for k in range(0, 8, 2):
        a, e = cols[k][k : k + 1], cols[k][k + 1 : k + 2]
        b, c = cols[k + 1][k : k + 1], cols[k + 1][k + 1 : k + 2]
        det = a * c - b * e
        inv = 1.0 / det
        logs = logs + jnp.log(det)
        ai, bi, ci, ei = a * inv, b * inv, c * inv, e * inv
        first, second = cols[k] - unit(k), cols[k + 1] - unit(k + 1)
        m0 = first * ci - second * ei
        m1 = second * ai - first * bi
        for j in range(8):
            if j == k:
                cols[j] = unit(k) - m0
            elif j == k + 1:
                cols[j] = unit(k + 1) - m1
            else:
                cols[j] = cols[j] - m0 * cols[j][k : k + 1] - m1 * cols[j][k + 1 : k + 2]
    return cols, logs


def inverse128(state, spread_ref):
    order = state.shape[0]
    lane = lax.broadcasted_iota(jnp.int32, (order, LANES), 1)
    row = lax.broadcasted_iota(jnp.int32, (order, LANES), 0)
    total = jnp.zeros((1, LANES), jnp.float32)
    for first in range(0, order, 8):
        last = first + 8
        cols = [jnp.broadcast_to(state[:, j : j + 1], (order, LANES)) for j in range(first, last)]
        for j in range(8):
            spread_ref[j] = cols[j][first:last]
        block, logs = inverse8([spread_ref[j] for j in range(8)])
        total = total + logs
        inside = (lane >= first) & (lane < last)
        cleared = jnp.where(inside, jnp.where(lane == row, 1.0, 0.0), state)
        scaled = block[0] * cleared[first : first + 1]
        for j in range(1, 8):
            scaled = scaled + block[j] * cleared[first + j : first + j + 1]
        rest = jnp.where(inside, 0.0, state)
        for j in range(8):
            rest = rest - cols[j] * scaled[j : j + 1]
        pieces = [rest[:first], scaled, rest[last:]]
        state = jnp.concatenate([piece for piece in pieces if piece.shape[0]], axis=0)
    return state, total


def gauss_jordan_half(matrix_ref, spread_ref, log_ref, j):
    half = matrix_ref.shape[0] // 2
    here = pl.ds(pl.multiple_of(j * half, half), half)
    there = pl.ds(pl.multiple_of((1 - j) * half, half), half)
    inv, logs = inverse128(matrix_ref[here, here], spread_ref)
    log_ref[...] += logs
    scaled = exact_dot(inv, matrix_ref[here, there])
    below = matrix_ref[there, here]
    matrix_ref[there, there] = matrix_ref[there, there] - exact_dot(below, scaled)
    matrix_ref[there, here] = -exact_dot(below, inv)
    matrix_ref[here, there] = scaled
    matrix_ref[here, here] = inv


def gauss_jordan(matrix_ref, spread_ref, log_ref, between):
    log_ref[...] = jnp.zeros_like(log_ref)

    def step(j, carry):
        gauss_jordan_half(matrix_ref, spread_ref, log_ref, j)
        if between is not None:
            pl.when(j == 0)(between)
        return carry

    lax.fori_loop(0, 2, step, 0)


def halves(value):
    high = value.astype(jnp.bfloat16)
    return high, (value - high.astype(jnp.float32)).astype(jnp.bfloat16)


def one_dot(left, right):
    return jnp.dot(left, right, preferred_element_type=jnp.float32)


def three_dot(left, right):
    (left_high, left_low), (right_high, right_low) = left, right
    return one_dot(left_high, right_high) + (one_dot(left_high, right_low) + one_dot(left_low, right_high))


def newton_start(level, inner, rest_ref, guess_ref):
    order = inner.shape[0]
    row = lax.broadcasted_iota(jnp.int32, (order, order), 0)
    lane = lax.broadcasted_iota(jnp.int32, (order, order), 1)
    eye = jnp.where(row == lane, 1.0, 0.0)
    cap = eye + inner
    spans = jnp.sum(jnp.abs(cap), axis=0, keepdims=True)
    largest = jnp.minimum(jnp.max(spans, axis=1, keepdims=True), 4.0 * 2**level + 1.0)
    scale = 2.0 / (1.0 + largest)
    rest = eye - cap * scale
    guess_ref[...] = (eye + rest) * scale
    parts = halves(rest)
    rest_ref[...] = three_dot(parts, parts)
    return largest, parts


def newton_round(rest_ref, guess_ref, _, carry):
    guess = guess_ref[...]
    parts = halves(rest_ref[...])
    guess_ref[...] = guess + three_dot(parts, halves(guess))
    rest_ref[...] = three_dot(parts, parts)
    return carry


LINE = 4


def near_far(level):
    near = min(2**level, 16)
    return near, 2**level // near


def near_peer(near, k):
    narrow, wide = lax.axis_index("narrow"), lax.axis_index("wide")
    here = lax.rem(wide, near)
    peer = lax.rem(here + k, near)
    return here, peer, (narrow, wide - here + peer)


def far_peer(far, k):
    narrow, wide = lax.axis_index("narrow"), lax.axis_index("wide")
    slab, inner = lax.div(wide, 16), lax.rem(wide, 16)
    index = slab if far <= 4 else narrow * 4 + slab
    here = lax.rem(index, far)
    peer = index - here + lax.rem(here + k, far)
    if far <= 4:
        return here, (narrow, peer * 16 + inner)
    return here, (lax.div(peer, 4), lax.rem(peer, 4) * 16 + inner)


def remote(src, dst, send_sem, recv_sem, device):
    return pltpu.make_async_remote_copy(
        src_ref=src, dst_ref=dst, send_sem=send_sem, recv_sem=recv_sem, device_id=device, device_id_type=MESH
    )


def hail(near, far):
    barrier = pltpu.get_barrier_semaphore()
    for k in range(1, near):
        pl.semaphore_signal(barrier, inc=1, device_id=near_peer(near, k)[2], device_id_type=MESH)
    for k in range(1, far):
        pl.semaphore_signal(barrier, inc=1, device_id=far_peer(far, k)[1], device_id_type=MESH)


def all_here(near, far):
    pl.semaphore_wait(pltpu.get_barrier_semaphore(), near + far - 2)


def column_peer(span, k):
    narrow, wide = lax.axis_index("narrow"), lax.axis_index("wide")
    index = lax.rem(lax.div(wide, LINE), span)
    peer = lax.rem(index + k, span)
    return index, peer, (narrow, wide + (peer - index) * LINE)


def prologue_kernel(
    points_ref, rights_ref, gram_ref, index_ref, points_out, rights_out, pair_out, upper_out, inv_out, log_out,
    inv, spread, rows, pair_landed, landed, passed, own, *sems,
):
    point_sems, right_sems, pair_sems, line_sems, inv_sems, column_sems, far_sems, near_sems = (
        sems[i : i + 2] for i in range(0, 16, 2)
    )
    near, far = near_far(7)
    hail(near, far)
    line = near_peer(LINE, 0)[0]
    column = column_peer(4, 0)[0]
    block = line * 4 + column
    all_here(near, far)
    first = []
    for k in range(1, LINE):
        device = near_peer(LINE, k)[2]
        first.append(
            remote(points_ref, points_out.at[line], point_sems[0].at[k - 1], point_sems[1].at[k - 1], device)
        )
        first[-1].start()
    late = []
    for k in range(1, LINE):
        device = near_peer(LINE, k)[2]
        late.append(
            remote(rights_ref, rights_out.at[line], right_sems[0].at[k - 1], right_sems[1].at[k - 1], device)
        )
        late[-1].start()
    points_out[line] = points_ref[...]
    rights_out[line] = rights_ref[...]
    inv[...] = gram_ref[...]
    for k in range(1, LINE):
        device = near_peer(LINE, k)[2]
        late.append(remote(inv, inv_out.at[line], inv_sems[0].at[k - 1], inv_sems[1].at[k - 1], device))
    pair = remote(rows.at[0], pair_landed, pair_sems[0].at[0], pair_sems[1].at[0], column_peer(2, 1)[2])
    copies = []
    for k in range(1, 4):
        _, peer, device = column_peer(4, k)
        copies.append(
            remote(
                rows.at[pl.ds(1, 4), peer], landed.at[k - 1], column_sems[0].at[k - 1], column_sems[1].at[k - 1], device
            )
        )

    def choose():
        for copy in first:
            copy.wait()
        index = index_ref[...]
        leaf = points_ref.shape[0]
        total = None
        for leaf_at in range(LINE):
            spot = lax.broadcasted_iota(jnp.int32, (index.shape[0], leaf), 1) + leaf_at * leaf
            term = one_dot(jnp.where(spot == index, 1.0, 0.0).astype(jnp.bfloat16), points_out[leaf_at])
            total = term if total is None else total + term
        rows[...] = total.astype(jnp.bfloat16).reshape(rows.shape)
        pair.start()
        for copy in copies:
            copy.start()

    gauss_jordan(inv, spread, log_out, choose)
    for copy in late[LINE - 1 :]:
        copy.start()
    inv_out[line] = inv[...]
    total = rows[pl.ds(1, 4), column].astype(jnp.float32)
    for k in range(1, 4):
        copies[k - 1].wait()
        total = total + landed[k - 1].astype(jnp.float32)
    own[...] = total.astype(jnp.bfloat16)
    copies = []
    for k in range(1, far):
        device = far_peer(far, k)[1]
        copies.append(
            remote(own.at[pl.ds(1, 3)], passed.at[k - 1], far_sems[0].at[k - 1], far_sems[1].at[k - 1], device)
        )
        copies[-1].start()
    pair.wait()
    pair_out[line] = (rows[0].astype(jnp.float32) + pair_landed[...].astype(jnp.float32)).astype(jnp.bfloat16)
    for k in range(1, LINE):
        mine = pair_out.at[line]
        late.append(remote(mine, mine, line_sems[0].at[k - 1], line_sems[1].at[k - 1], near_peer(LINE, k)[2]))
        late[-1].start()
    position = far_peer(far, 0)[0]
    sums = [total[1], total[2], total[3]]
    for k in range(1, far):
        copies[k - 1].wait()
        sender = lax.rem(position + far - k, far)
        core = lax.div(sender, 4) == lax.div(position, 4)
        slab = lax.div(sender, 2) == lax.div(position, 2)
        keep = [jnp.where(slab, 1.0, 0.0), jnp.where(core, 1.0, 0.0), 1.0]
        for i in range(3):
            sums[i] = sums[i] + passed[k - 1, i].astype(jnp.float32) * keep[i]
    upper_out[0, block] = total[0].astype(jnp.bfloat16)
    for i in range(3):
        upper_out[i + 1, block] = sums[i].astype(jnp.bfloat16)
    for k in range(1, near):
        mine = upper_out.at[:, block]
        late.append(remote(mine, mine, near_sems[0].at[k - 1], near_sems[1].at[k - 1], near_peer(near, k)[2]))
        late[-1].start()
    for copy in late:
        copy.wait()


def prologue(points, rights, gram, index):
    leaf, width = points.shape
    order = gram.shape[0]
    near, far = near_far(7)
    few = index.shape[0] // 20
    dma = pltpu.SemaphoreType.DMA
    counts = [LINE - 1, LINE - 1, 1, LINE - 1, LINE - 1, 3, far - 1, near - 1]
    return pl.pallas_call(
        prologue_kernel,
        out_shape=(
            jax.ShapeDtypeStruct((LINE, leaf, width), jnp.bfloat16),
            jax.ShapeDtypeStruct((LINE, *rights.shape), jnp.float32),
            jax.ShapeDtypeStruct((LINE, 4, few, width), jnp.bfloat16),
            jax.ShapeDtypeStruct((4, near, few, width), jnp.bfloat16),
            jax.ShapeDtypeStruct((LINE, order, order), jnp.float32),
            jax.ShapeDtypeStruct((1, LANES), jnp.float32),
        ),
        in_specs=[pl.BlockSpec(memory_space=VMEM)] * 4,
        out_specs=(pl.BlockSpec(memory_space=VMEM),) * 6,
        scratch_shapes=[
            VMEM((order, order), jnp.float32),
            VMEM((8, 8, LANES), jnp.float32),
            VMEM((5, 4, few, width), jnp.bfloat16),
            VMEM((4, few, width), jnp.bfloat16),
            VMEM((3, 4, few, width), jnp.bfloat16),
            VMEM((far - 1, 3, few, width), jnp.bfloat16),
            VMEM((4, few, width), jnp.bfloat16),
            *[dma((count,)) for count in counts for _ in range(2)],
        ],
        compiler_params=pltpu.CompilerParams(collective_id=1, has_side_effects=True),
        name="prologue",
    )(points, rights, gram, index)


def level_shapes(level, order, width):
    near, far = near_far(level)
    span = near // LINE
    rows = order // near
    left = width - (level - 1) * order
    shapes = [VMEM((order, left), jnp.bfloat16)]
    for size in (order, left - order):
        shapes.append(VMEM((span - 1, rows, size), jnp.bfloat16))
        if far > 1:
            shapes += [VMEM((far - 1, rows, size), jnp.bfloat16), VMEM((rows, size), jnp.bfloat16)]
    counts = [span - 1, span - 1, near - 1, near - 1] + ([far - 1, far - 1] if far > 1 else [])
    return shapes + [pltpu.SemaphoreType.DMA((count,)) for count in counts * 2]


class LevelSum:
    def __init__(self, level, part_ref, refs):
        self.near, self.far = near_far(level)
        self.span = self.near // LINE
        self.part, self.sums = part_ref, refs[0]
        order, left = self.sums.shape
        self.rows = order // self.near
        self.start = (level - 1) * order
        self.pieces = ((0, order), (order, left - order))
        many = 3 if self.far > 1 else 1
        self.buffers = (refs[1 : 1 + many], refs[1 + many : 1 + 2 * many])
        sems = refs[1 + 2 * many :]
        self.sems = (sems[: len(sems) // 2], sems[len(sems) // 2 :])
        self.line = near_peer(LINE, 0)[0]
        self.column = column_peer(self.span, 0)[0]

    def block(self, column):
        return pl.ds(pl.multiple_of((self.line * self.span + column) * self.rows, self.rows), self.rows)

    def from_part(self, i, column):
        first, size = self.pieces[i]
        return self.part.at[self.block(column), pl.ds(self.start + first, size)]

    def scatter(self, i):
        send, recv = self.sems[i][:2]
        copies = []
        for k in range(1, self.span):
            _, peer, device = column_peer(self.span, k)
            landed = self.buffers[i][0].at[k - 1]
            copies.append(remote(self.from_part(i, peer), landed, send.at[k - 1], recv.at[k - 1], device))
            copies[-1].start()
        return copies

    def add_up(self, i, copies):
        total = self.from_part(i, self.column)[...].astype(jnp.float32)
        for k in range(1, self.span):
            copies[k - 1].wait()
            total = total + self.buffers[i][0][k - 1].astype(jnp.float32)
        return total

    def pass_on(self, i, total):
        _, passed, own = self.buffers[i]
        send, recv = self.sems[i][4:6]
        own[...] = total.astype(jnp.bfloat16)
        copies = []
        for k in range(1, self.far):
            device = far_peer(self.far, k)[1]
            copies.append(remote(own, passed.at[k - 1], send.at[k - 1], recv.at[k - 1], device))
            copies[-1].start()
        return copies

    def add_far(self, i, copies):
        _, passed, own = self.buffers[i]
        total = own[...].astype(jnp.float32)
        for k in range(1, self.far):
            copies[k - 1].wait()
            total = total + passed[k - 1].astype(jnp.float32)
        return total

    def gather(self, i, total):
        first, size = self.pieces[i]
        mine = self.sums.at[self.block(self.column), pl.ds(first, size)]
        mine[...] = total.astype(jnp.bfloat16)
        send, recv = self.sems[i][2:4]
        copies = []
        for k in range(1, self.near):
            copies.append(remote(mine, mine, send.at[k - 1], recv.at[k - 1], near_peer(self.near, k)[2]))
            copies[-1].start()
        return copies


def tree_kernel(levels, first_ref, bases_ref, rights_ref, inv_ref, targets_ref, log_ref, answer_out, totals_out, *refs):
    solved, answer, basis_coef, target_coef, part, base_t, rest, guess, cap, spread, logs = refs[:11]
    last = refs[11:19]
    level_refs, at = {}, 19
    order, width = part.shape
    for level in range(3, levels + 1):
        count = len(level_shapes(level, order, width))
        level_refs[level] = refs[at : at + count]
        at += count
    leaf = inv_ref.shape[1]
    tail = levels * order
    near, far = near_far(levels)
    device = lax.axis_index("narrow") * lax.axis_size("wide") + lax.axis_index("wide")
    spot = lax.rem(device, LINE)
    hail(near, far)

    def columns(c):
        return pl.ds(pl.multiple_of(c * order, order), order)

    def leaf_solve(j, carry):
        rows = pl.ds(pl.multiple_of(j * leaf, leaf), leaf)
        inverse = inv_ref[j]
        parts = halves(inverse)
        answer[rows] = exact_dot(inverse, rights_ref[j])
        solved[rows, :order] = three_dot(parts, halves(first_ref[rows])).astype(jnp.bfloat16)

        def chunk(c, carry):
            right = bases_ref[rows, columns(c - 1)]
            solved[rows, columns(c)] = three_dot(halves(inv_ref[j]), halves(right)).astype(jnp.bfloat16)
            return carry

        return lax.fori_loop(1, levels, chunk, carry)

    lax.fori_loop(0, LINE, leaf_solve, 0)
    cap[...] = jnp.zeros_like(cap)

    def choose_cap(inner, mine):
        keep = jnp.where(mine, 1.0, 0.0)
        cap[...] = inner * keep + cap[...] * (1.0 - keep)

    def invert(level, inner):
        newton_start(level, inner, rest, guess)
        lax.fori_loop(0, level + 4, functools.partial(newton_round, rest, guess), 0)

    def products(base, rows, level):
        high, low = halves(base.T)
        base_t[:, : base.shape[0]] = high
        part[:, tail:] = three_dot((high, low), halves(answer[rows])).astype(jnp.bfloat16)

        def chunk(c, carry):
            left = base_t[:, : base.shape[0]]
            part[:, columns(c)] = one_dot(left, solved[rows, columns(c)]).astype(jnp.bfloat16)
            return carry

        lax.fori_loop(level - 1, levels, chunk, 0)

    def solve(level, sums, first, target):
        high, low = halves(guess[...])
        right = sums[:, target:]
        target_coef[...] = one_dot(high, right) + one_dot(low, right)

        def chunk(c, carry):
            right = sums[:, pl.ds(pl.multiple_of(first + (c - level) * order, LANES), order)]
            high, low = halves(guess[...])
            basis_coef[:, columns(c)] = (one_dot(high, right) + one_dot(low, right)).astype(jnp.bfloat16)
            return carry

        lax.fori_loop(level, levels, chunk, 0)

    def take_out_targets(level, rows):
        front = solved[rows, (level - 1) * order : level * order]
        high, low = halves(target_coef[...])
        return answer[rows] - (one_dot(front, high) + one_dot(front, low))

    def take_out(level, rows, c):
        front = solved[rows, (level - 1) * order : level * order]
        old = solved[rows, columns(c)].astype(jnp.float32)
        new = (old - one_dot(front, basis_coef[:, columns(c)])).astype(jnp.bfloat16)
        solved[rows, columns(c)] = new
        return new

    def pair_level(pair, carry):
        rows = pl.ds(pl.multiple_of(pair * 2 * leaf, leaf), 2 * leaf)
        products(first_ref[rows], rows, 1)
        inner = part[:, :order].astype(jnp.float32)
        choose_cap(inner, (pair == lax.div(spot, 2)) & (lax.rem(device, 2) == 1))
        invert(1, inner)
        solve(1, part, order, tail)
        answer[rows] = take_out_targets(1, rows)

        def chunk(c, carry):
            take_out(1, rows, c)
            return carry

        return lax.fori_loop(1, levels, chunk, carry)

    lax.fori_loop(0, 2, pair_level, 0)
    everything = pl.ds(0, LINE * leaf)
    products(bases_ref[:, :order], everything, 2)
    inner = part[:, order : 2 * order].astype(jnp.float32)
    choose_cap(inner, lax.rem(device, 4) == 2)
    invert(2, inner)
    solve(2, part, 2 * order, tail)

    for level in range(3, levels + 1):
        sums = LevelSum(level, part, level_refs[level])
        base_high, base_low = halves(bases_ref[:, (level - 2) * order : (level - 1) * order].T)
        base_t[...] = base_high

        def update(c, carry):
            new = take_out(level - 1, everything, c)
            part[:, columns(c)] = one_dot(base_t[...], new).astype(jnp.bfloat16)
            return carry

        update(level - 1, 0)
        if level == 3:
            all_here(near, far)
        ahead = sums.scatter(0)
        left = take_out_targets(level - 1, everything)
        answer[...] = left
        part[:, tail:] = three_dot((base_high, base_low), halves(left)).astype(jnp.bfloat16)
        lax.fori_loop(level, levels, update, 0)
        behind = sums.scatter(1)
        if sums.far > 1:
            ahead = sums.pass_on(0, sums.add_up(0, ahead))
            behind = sums.pass_on(1, sums.add_up(1, behind))
            ahead = sums.gather(0, sums.add_far(0, ahead))
            behind = sums.gather(1, sums.add_far(1, behind))
        else:
            ahead = sums.gather(0, sums.add_up(0, ahead))
            behind = sums.gather(1, sums.add_up(1, behind))
        for copy in ahead:
            copy.wait()
        inner = sums.sums[:, :order].astype(jnp.float32)
        choose_cap(inner, lax.rem(device, 2**level) == 2 ** (level - 1))
        invert(level, inner)
        for copy in behind:
            copy.wait()
        solve(level, sums.sums, order, tail - (level - 1) * order)

    own_rows = pl.ds(pl.multiple_of(spot * leaf, leaf), leaf)
    own_answer = take_out_targets(levels, own_rows)
    answer_out[...] = own_answer

    landed, passed, terms, own, near_send, near_recv, far_send, far_recv = last
    row = lax.broadcasted_iota(jnp.int32, (order, order), 0)
    lane = lax.broadcasted_iota(jnp.int32, (order, order), 1)
    cap[...] = cap[...] + jnp.where(row == lane, 1.0, 0.0)
    gauss_jordan(cap, spread, logs, None)
    fits = jnp.sum(targets_ref[...] * own_answer, axis=0, keepdims=True)
    line = lax.broadcasted_iota(jnp.int32, terms.shape, 0)
    terms[...] = jnp.where(line == 0, fits, jnp.where(line == 1, logs[...] + log_ref[...], 0.0))
    here = near_peer(near, 0)[0]
    copies = []
    for k in range(1, near):
        device = near_peer(near, k)[2]
        copies.append(remote(terms, landed.at[here], near_send.at[k - 1], near_recv.at[k - 1], device))
        copies[-1].start()
    landed[here] = terms[...]
    for copy in copies:
        copy.wait()
    total = landed[0]
    for k in range(1, near):
        total = total + landed[k]
    own[...] = total
    index = far_peer(far, 0)[0]
    copies = []
    for k in range(1, far):
        copies.append(remote(own, passed.at[index], far_send.at[k - 1], far_recv.at[k - 1], far_peer(far, k)[1]))
        copies[-1].start()
    passed[index] = total
    for copy in copies:
        copy.wait()
    total = passed[0]
    for k in range(1, far):
        total = total + passed[k]
    totals_out[...] = total


def tree(first_base, bases, rights, inverses, targets, leaf_log, levels):
    points, order = first_base.shape
    width = levels * order + LANES
    near, far = near_far(levels)
    dma = pltpu.SemaphoreType.DMA
    terms = (8, LANES)
    scratch = [
        VMEM((points, levels * order), jnp.bfloat16),
        VMEM((points, LANES), jnp.float32),
        VMEM((order, levels * order), jnp.bfloat16),
        VMEM((order, LANES), jnp.float32),
        VMEM((order, width), jnp.bfloat16),
        VMEM((order, points), jnp.bfloat16),
        VMEM((order, order), jnp.float32),
        VMEM((order, order), jnp.float32),
        VMEM((order, order), jnp.float32),
        VMEM((8, 8, LANES), jnp.float32),
        VMEM((1, LANES), jnp.float32),
        VMEM((near, *terms), jnp.float32),
        VMEM((far, *terms), jnp.float32),
        VMEM(terms, jnp.float32),
        VMEM(terms, jnp.float32),
        *[dma((count - 1,)) for count in (near, near, far, far)],
    ]
    for level in range(3, levels + 1):
        scratch += level_shapes(level, order, width)
    return pl.pallas_call(
        functools.partial(tree_kernel, levels),
        out_shape=(jax.ShapeDtypeStruct(targets.shape, jnp.float32), jax.ShapeDtypeStruct(terms, jnp.float32)),
        in_specs=[pl.BlockSpec(memory_space=VMEM)] * 6,
        out_specs=(pl.BlockSpec(memory_space=VMEM),) * 2,
        scratch_shapes=scratch,
        compiler_params=pltpu.CompilerParams(
            collective_id=2, has_side_effects=True, vmem_limit_bytes=56 * 2**20
        ),
        name="tree",
    )(first_base, bases, rights, inverses, targets, leaf_log)


def kern(left, right):
    left_sq = jnp.sum(jnp.square(left.astype(jnp.float32)), axis=-1)
    right_sq = jnp.sum(jnp.square(right.astype(jnp.float32)), axis=-1)
    cross = jnp.einsum("...iw,...jw->...ij", left, right, preferred_element_type=jnp.float32)
    return jnp.exp(-(left_sq[..., :, None] + right_sq[..., None, :] - 2.0 * cross) / left.shape[-1])


def pick(points, index):
    chosen = (index[:, None] == jnp.arange(points.shape[0], dtype=jnp.int32)[None, :]).astype(jnp.bfloat16)
    return jnp.dot(chosen, points, preferred_element_type=jnp.float32).astype(jnp.bfloat16)


def per_device(embeddings, noise, targets, level_scale, skeleton):
    leaf, width = embeddings.shape
    levels, _, rank = skeleton.shape
    rhs = targets.shape[1]
    wide_size = lax.axis_size("wide")
    device = lax.axis_index("narrow") * wide_size + lax.axis_index("wide")
    spot = lax.rem(device, LINE)
    quarter = rank // LINE
    scales = jnp.sqrt(level_scale / rank)

    gram = kern(embeddings, embeddings) + jnp.diag(noise)
    local = skeleton[:, 0, :] - (device - spot) * leaf
    padded = jnp.pad(targets, ((0, 0), (0, LANES - rhs))).at[:, rhs].set(local[0].astype(jnp.float32))
    own_rows = lax.dynamic_slice(local[2:], (0, spot * quarter), (levels - 2, quarter))
    blocks, rights, third_centers, upper_centers, inverses, leaf_log = prologue(
        embeddings, padded, gram, own_rows.reshape(-1, 1)
    )
    points = blocks.reshape(LINE * leaf, width)
    pair_index = rights[::2, :, rhs].astype(jnp.int32)
    low = pick(points, jnp.concatenate([pair_index.reshape(-1), local[1]]))
    shared_centers = jnp.concatenate(
        [low[2 * rank :], third_centers.reshape(rank, width), upper_centers.reshape((levels - 3) * rank, width)]
    )
    first_base = kern(blocks.reshape(2, 2 * leaf, width), low[: 2 * rank].reshape(2, rank, width)) * scales[0]
    bases = kern(points, shared_centers) * jnp.repeat(scales[1:], rank)[None, :]
    answer, totals = tree(
        first_base.reshape(LINE * leaf, rank), bases, rights, inverses, padded, leaf_log, levels
    )
    answer = answer[:, :rhs]
    npoints = leaf * lax.axis_size("narrow") * wide_size
    return (answer, totals[0, :rhs] / npoints, totals[1, 0] / npoints)


def solution(mesh):
    return jax.shard_map(
        per_device,
        mesh=mesh,
        in_specs=(
            P(NARROW_WIDE, None),
            P(NARROW_WIDE),
            P(NARROW_WIDE, None),
            P(),
            P(None, NARROW_WIDE, None),
        ),
        out_specs=(P(NARROW_WIDE, None), P(), P()),
        check_vma=False,
    )
```

profile of v0, /device:TPU:1, one launch (start us, length us, event | category | flops | bytes accessed | tf_op | source)
XLA Modules:
  0.0 216.3 jit_solution(14087016085537190551)
XLA Ops:
  0.6 0.0 copy-start.2
  0.7 0.7 broadcast_subtract_fusion
  1.4 0.1 dynamic-slice_reduce_fusion
  1.5 0.8 reshape.110.index_ref
  2.3 0.6 compare_reduce_fusion
  2.9 0.6 fusion.13
  3.6 0.1 copy.11
  3.7 0.9 copy.10
  4.7 0.6 scatter.4.rights_ref.targets_ref
  5.3 0.0 copy-start
  5.3 1.1 multiply_reduce_fusion.3
  6.4 1.9 fusion.12.gram_ref
  8.3 0.0 copy-done
  8.3 41.3 %prologue.1 = (bf16[4,256,256]{2,1,0:T(8,128)(2,1)}, f32[4,256,128]{2,1,0:T(8,128)}, bf16[4,4,16,256]{3,2,1,0:T(8,128)(2,1)}, bf16[4,16,16,256]{3,2,1,0:T(8,128)...) custom-call(bf16[256,256]{1,0:T(8,128)(2,1)} %points_ref.1, f32[256,128]{1,0:T(8,128)} %copy-done, ...), custom_call_target="tpu_custom_call" | custom-call | tf_op jit(solution)/shard_map/prologue/pallas_call | solution.py:297
  49.6 1.2 convert_reduce_fusion
  50.9 1.7 fusion.7
  52.6 1.3 multiply_reduce_fusion
  53.9 1.3 multiply_reduce_fusion.1
  55.2 0.0 copy-done.2
  55.2 0.1 slice.58
  55.3 0.1 broadcast_in_dim.31
  55.4 0.0 copy-start.1
  55.4 5.6 %exponential_multiply_fusion.bases_ref = f32[1024,1536]{1,0:T(8,128)} fusion(bf16[1024,256]{1,0:T(8,128)(2,1)} %bitcast.29, f32[1536]{0:T(1024)S(1)} %mul.54, f32[1536]{0:T(1024)S(1)} %multiply_reduce_fusion, f32[1024]{0:T(1024)S(1)} %bitcast.39, bf16[1024,256]{1,0:T(8,128)(2,1)} %bitcast.27, bf16[256,256]{1,0:T(8,128)(2,1)} %bitcast.33, ...), kind=kOutput, calls=%fused_computation | convolution fusion | flops 817102848 | bytes 7618560 | tf_op jit(solution)/shard_map/...iw,...jw->...ij/dot_general | solution.py:630
  61.0 0.1 multiply_reduce_fusion.2
  61.2 0.0 copy-done.1
  61.2 1.4 fusion.6
  62.7 147.9 %tree.1 = (f32[256,128]{1,0:T(8,128)}, f32[8,128]{1,0:T(8,128)}) custom-call(f32[1024,256]{1,0:T(8,128)} %bitcast.25, f32[1024,1536]{1,0:T(8,128)} %exponential_multiply_fusion.bases_ref, f32[4,256,128]{2,1,0:T(8,128)} %get-tuple-element.24.rights_ref, f32[4,256,256]{2,1,0:T(8,128)} %get-tuple-element.27.inv_ref, f32[256,128]{1,0:T(8,128)} %copy-done, ...), custom_call_target="tpu_custom_call" | custom-call | tf_op jit(solution)/shard_map/tree/pallas_call | solution.py:614
  210.5 1.6 copy.13
  212.1 1.2 slice.61
  214.0 1.2 multiply_bitcast_fusion
  (12 shorter events, 0.1 us)
Async XLA Ops:
  0.6 54.6 %copy-start.2 = (f32[7]{0:T(128)S(1)}, f32[7]{0:T(128)}, u32[]{:S(2)}) copy-start(f32[7]{0:T(128)} %param.10) | copy-start | bytes 88
  5.3 3.0 %copy-start = (f32[256,128]{1,0:T(8,128)}, f32[256,128]{1,0:T(8,128)S(1)}, u32[]{:S(2)}) copy-start(f32[256,128]{1,0:T(8,128)S(1)} %scatter.4.rights_ref.targets_ref) | copy-start | bytes 393220
  55.4 5.8 %copy-start.1 = (bf16[4,256,256]{2,1,0:T(8,128)(2,1)S(1)}, bf16[4,256,256]{2,1,0:T(8,128)(2,1)}, u32[]{:S(2)}) copy-start(bf16[4,256,256]{2,1,0:T(8,128)(2,1)} %get-tuple-element.23) | copy-start | bytes 1572868
where the time goes:
time: 217 us; the launch traced here: 216 us
  Pallas kernels  189 us (87%)
  matrix products  10.7 us (5%)
  other arithmetic  8.22 us (4%)
  local copies, waits for them, and re-layouts  5.64 us (3%)
  between operations  2.58 us (1%)
    pallas_call x1, Pallas kernels, tree(): pl.pallas_call(functools.partial(tree_kernel, levels), out_shape=(jax.Sha...  148 us
    pallas_call x1, Pallas kernels, prologue(): pl.pallas_call(prologue_kernel, out_shape=(jax.ShapeDtypeStruct((LINE, le...  41.3 us
    dot_general x3, matrix products, kern(): jnp.einsum('...iw,...jw->...ij', left, right, preferred_element_type=jnp....  8.99 us

commit v1 on v0

--- a/solution.py
+++ b/solution.py
@@ -46,7 +46,7 @@
     return cols, logs
 
 
-def inverse128(state, spread_ref):
+def inverse128(state, spread_ref, beside):
     order = state.shape[0]
     lane = lax.broadcasted_iota(jnp.int32, (order, LANES), 1)
     row = lax.broadcasted_iota(jnp.int32, (order, LANES), 0)
@@ -66,16 +66,18 @@
         rest = jnp.where(inside, 0.0, state)
         for j in range(8):
             rest = rest - cols[j] * scaled[j : j + 1]
+        if beside is not None and first % 16 == 8 and first < 96:
+            beside()
         pieces = [rest[:first], scaled, rest[last:]]
         state = jnp.concatenate([piece for piece in pieces if piece.shape[0]], axis=0)
     return state, total
 
 
-def gauss_jordan_half(matrix_ref, spread_ref, log_ref, j):
+def gauss_jordan_half(matrix_ref, spread_ref, log_ref, j, beside):
     half = matrix_ref.shape[0] // 2
     here = pl.ds(pl.multiple_of(j * half, half), half)
     there = pl.ds(pl.multiple_of((1 - j) * half, half), half)
-    inv, logs = inverse128(matrix_ref[here, here], spread_ref)
+    inv, logs = inverse128(matrix_ref[here, here], spread_ref, beside)
     log_ref[...] += logs
     scaled = exact_dot(inv, matrix_ref[here, there])
     below = matrix_ref[there, here]
@@ -85,11 +87,11 @@
     matrix_ref[here, here] = inv
 
 
-def gauss_jordan(matrix_ref, spread_ref, log_ref, between):
+def gauss_jordan(matrix_ref, spread_ref, log_ref, between=None, beside=None):
     log_ref[...] = jnp.zeros_like(log_ref)
 
     def step(j, carry):
-        gauss_jordan_half(matrix_ref, spread_ref, log_ref, j)
+        gauss_jordan_half(matrix_ref, spread_ref, log_ref, j, beside)
         if between is not None:
             pl.when(j == 0)(between)
         return carry
@@ -108,7 +110,10 @@
 
 def three_dot(left, right):
     (left_high, left_low), (right_high, right_low) = left, right
-    return one_dot(left_high, right_high) + (one_dot(left_high, right_low) + one_dot(left_low, right_high))
+    return one_dot(
+        jnp.concatenate([left_high, left_high, left_low], axis=1),
+        jnp.concatenate([right_high, right_low, right_high], axis=0),
+    )
 
 
 def newton_start(level, inner, rest_ref, guess_ref):
@@ -186,39 +191,62 @@
     return index, peer, (narrow, wide + (peer - index) * LINE)
 
 
-def prologue_kernel(
-    points_ref, rights_ref, gram_ref, index_ref, points_out, rights_out, pair_out, upper_out, inv_out, log_out,
-    inv, spread, rows, pair_landed, landed, passed, own, *sems,
-):
+def kernel_values(left, right):
+    wide_left, wide_right = left.astype(jnp.float32), right.astype(jnp.float32)
+    left_sq = jnp.sum(wide_left * wide_left, axis=1, keepdims=True)
+    turned = (((1,), (1,)), ((), ()))
+    ones = jnp.ones((8, right.shape[1]), jnp.float32)
+    right_sq = lax.dot_general(
+        ones, wide_right * wide_right, turned, precision=EXACT, preferred_element_type=jnp.float32
+    )[0:1]
+    cross = lax.dot_general(left, right, turned, preferred_element_type=jnp.float32)
+    return jnp.exp(-(left_sq + right_sq - 2.0 * cross) / left.shape[1])
+
+
+def rows_at(points, index):
+    leaf = points.shape[1]
+    total = None
+    for leaf_at in range(LINE):
+        spot = lax.broadcasted_iota(jnp.int32, (index.shape[0], leaf), 1) + leaf_at * leaf
+        term = one_dot(jnp.where(spot == index, 1.0, 0.0).astype(jnp.bfloat16), points[leaf_at])
+        total = term if total is None else total + term
+    return total.astype(jnp.bfloat16)
+
+
+PROLOGUE_COUNTS = [3, 3, 1, 3, 3, 3, 7, 15]
+
+
+def prologue(points_ref, rights_ref, noise_ref, index_ref, scales_ref, rights, inv_all, first, bases, log, refs):
+    inv, spread, points, pair_all, upper, rows, low, pair_landed, landed, passed, own = refs[:11]
+    sems = refs[11:]
     point_sems, right_sems, pair_sems, line_sems, inv_sems, column_sems, far_sems, near_sems = (
         sems[i : i + 2] for i in range(0, 16, 2)
     )
     near, far = near_far(7)
-    hail(near, far)
     line = near_peer(LINE, 0)[0]
     column = column_peer(4, 0)[0]
     block = line * 4 + column
+    leaf = points_ref.shape[0]
+    order = inv.shape[0]
+
+    def to_line(source, target, pair_of_sems):
+        send, recv = pair_of_sems
+        return [
+            remote(source, target, send.at[k - 1], recv.at[k - 1], near_peer(LINE, k)[2]) for k in range(1, LINE)
+        ]
+
+    row = lax.broadcasted_iota(jnp.int32, (order, order), 0)
+    lane = lax.broadcasted_iota(jnp.int32, (order, order), 1)
+    own_points = points_ref[...]
+    inv[...] = kernel_values(own_points, own_points) + jnp.where(row == lane, noise_ref[...], 0.0)
     all_here(near, far)
-    first = []
-    for k in range(1, LINE):
-        device = near_peer(LINE, k)[2]
-        first.append(
-            remote(points_ref, points_out.at[line], point_sems[0].at[k - 1], point_sems[1].at[k - 1], device)
-        )
-        first[-1].start()
-    late = []
-    for k in range(1, LINE):
-        device = near_peer(LINE, k)[2]
-        late.append(
-            remote(rights_ref, rights_out.at[line], right_sems[0].at[k - 1], right_sems[1].at[k - 1], device)
-        )
-        late[-1].start()
-    points_out[line] = points_ref[...]
-    rights_out[line] = rights_ref[...]
-    inv[...] = gram_ref[...]
-    for k in range(1, LINE):
-        device = near_peer(LINE, k)[2]
-        late.append(remote(inv, inv_out.at[line], inv_sems[0].at[k - 1], inv_sems[1].at[k - 1], device))
+    points_copies = to_line(points_ref, points.at[line], point_sems)
+    rights_copies = to_line(rights_ref, rights.at[line], right_sems)
+    for copy in points_copies + rights_copies:
+        copy.start()
+    points[line] = own_points
+    rights[line] = rights_ref[...]
+    inv_copies = to_line(inv, inv_all.at[line], inv_sems)
     pair = remote(rows.at[0], pair_landed, pair_sems[0].at[0], pair_sems[1].at[0], column_peer(2, 1)[2])
     copies = []
     for k in range(1, 4):
@@ -230,24 +258,14 @@
         )
 
     def choose():
-        for copy in first:
+        for copy in points_copies:
             copy.wait()
-        index = index_ref[...]
-        leaf = points_ref.shape[0]
-        total = None
-        for leaf_at in range(LINE):
-            spot = lax.broadcasted_iota(jnp.int32, (index.shape[0], leaf), 1) + leaf_at * leaf
-            term = one_dot(jnp.where(spot == index, 1.0, 0.0).astype(jnp.bfloat16), points_out[leaf_at])
-            total = term if total is None else total + term
-        rows[...] = total.astype(jnp.bfloat16).reshape(rows.shape)
+        rows[...] = rows_at(points, index_ref[order:]).reshape(rows.shape)
         pair.start()
         for copy in copies:
             copy.start()
 
-    gauss_jordan(inv, spread, log_out, choose)
-    for copy in late[LINE - 1 :]:
-        copy.start()
-    inv_out[line] = inv[...]
+    gauss_jordan(inv, spread, log, between=choose)
     total = rows[pl.ds(1, 4), column].astype(jnp.float32)
     for k in range(1, 4):
         copies[k - 1].wait()
@@ -261,11 +279,29 @@
         )
         copies[-1].start()
     pair.wait()
-    pair_out[line] = (rows[0].astype(jnp.float32) + pair_landed[...].astype(jnp.float32)).astype(jnp.bfloat16)
-    for k in range(1, LINE):
-        mine = pair_out.at[line]
-        late.append(remote(mine, mine, line_sems[0].at[k - 1], line_sems[1].at[k - 1], near_peer(LINE, k)[2]))
-        late[-1].start()
+    pair_all[line] = (rows[0].astype(jnp.float32) + pair_landed[...].astype(jnp.float32)).astype(jnp.bfloat16)
+    line_copies = to_line(pair_all.at[line], pair_all.at[line], line_sems)
+    for copy in line_copies + inv_copies:
+        copy.start()
+    inv_all[line] = inv[...]
+
+    def base(level, centers, leaf_at):
+        values = kernel_values(points[leaf_at], centers) * scales_ref[level - 1]
+        here = pl.ds(pl.multiple_of(leaf_at * leaf, leaf), leaf)
+        if level == 1:
+            first[here] = values
+        else:
+            bases[here, (level - 2) * order : (level - 1) * order] = values
+
+    def base_everywhere(level, centers):
+        def one(leaf_at, carry):
+            base(level, low[...], leaf_at)
+            return carry
+
+        low[...] = centers
+        lax.fori_loop(0, LINE, one, 0)
+
+    base_everywhere(2, rows_at(points, index_ref[:order]))
     position = far_peer(far, 0)[0]
     sums = [total[1], total[2], total[3]]
     for k in range(1, far):
@@ -276,56 +312,61 @@
         keep = [jnp.where(slab, 1.0, 0.0), jnp.where(core, 1.0, 0.0), 1.0]
         for i in range(3):
             sums[i] = sums[i] + passed[k - 1, i].astype(jnp.float32) * keep[i]
-    upper_out[0, block] = total[0].astype(jnp.bfloat16)
+    upper[0, block] = total[0].astype(jnp.bfloat16)
     for i in range(3):
-        upper_out[i + 1, block] = sums[i].astype(jnp.bfloat16)
+        upper[i + 1, block] = sums[i].astype(jnp.bfloat16)
+    near_copies = []
     for k in range(1, near):
-        mine = upper_out.at[:, block]
-        late.append(remote(mine, mine, near_sems[0].at[k - 1], near_sems[1].at[k - 1], near_peer(near, k)[2]))
-        late[-1].start()
-    for copy in late:
+        mine = upper.at[:, block]
+        near_copies.append(remote(mine, mine, near_sems[0].at[k - 1], near_sems[1].at[k - 1], near_peer(near, k)[2]))
+        near_copies[-1].start()
+    for copy in rights_copies:
         copy.wait()
-
-
-def prologue(points, rights, gram, index):
-    leaf, width = points.shape
-    order = gram.shape[0]
+    column_of_index = rights_ref.shape[1] // 2
+
+    def pair_base(pair, carry):
+        index = rights[2 * pair, :, column_of_index : column_of_index + 1].astype(jnp.int32)
+        low[...] = rows_at(points, index)
+        base(1, low[...], 2 * pair)
+        base(1, low[...], 2 * pair + 1)
+        return carry
+
+    lax.fori_loop(0, 2, pair_base, 0)
+    for copy in line_copies:
+        copy.wait()
+    base_everywhere(3, pair_all[...].reshape(order, -1))
+    for copy in near_copies:
+        copy.wait()
+    for level in range(4, 8):
+        base_everywhere(level, upper[level - 4].reshape(order, -1))
+    for copy in inv_copies:
+        copy.wait()
+
+
+def prologue_shapes(leaf, width, order):
+    few = order // 16
     near, far = near_far(7)
-    few = index.shape[0] // 20
-    dma = pltpu.SemaphoreType.DMA
-    counts = [LINE - 1, LINE - 1, 1, LINE - 1, LINE - 1, 3, far - 1, near - 1]
-    return pl.pallas_call(
-        prologue_kernel,
-        out_shape=(
-            jax.ShapeDtypeStruct((LINE, leaf, width), jnp.bfloat16),
-            jax.ShapeDtypeStruct((LINE, *rights.shape), jnp.float32),
-            jax.ShapeDtypeStruct((LINE, 4, few, width), jnp.bfloat16),
-            jax.ShapeDtypeStruct((4, near, few, width), jnp.bfloat16),
-            jax.ShapeDtypeStruct((LINE, order, order), jnp.float32),
-            jax.ShapeDtypeStruct((1, LANES), jnp.float32),
-        ),
-        in_specs=[pl.BlockSpec(memory_space=VMEM)] * 4,
-        out_specs=(pl.BlockSpec(memory_space=VMEM),) * 6,
-        scratch_shapes=[
-            VMEM((order, order), jnp.float32),
-            VMEM((8, 8, LANES), jnp.float32),
-            VMEM((5, 4, few, width), jnp.bfloat16),
-            VMEM((4, few, width), jnp.bfloat16),
-            VMEM((3, 4, few, width), jnp.bfloat16),
-            VMEM((far - 1, 3, few, width), jnp.bfloat16),
-            VMEM((4, few, width), jnp.bfloat16),
-            *[dma((count,)) for count in counts for _ in range(2)],
-        ],
-        compiler_params=pltpu.CompilerParams(collective_id=1, has_side_effects=True),
-        name="prologue",
-    )(points, rights, gram, index)
-
-
-def level_shapes(level, order, width):
+    bf16 = jnp.bfloat16
+    return [
+        VMEM((order, order), jnp.float32),
+        VMEM((8, 8, LANES), jnp.float32),
+        VMEM((LINE, leaf, width), bf16),
+        VMEM((LINE, 4, few, width), bf16),
+        VMEM((4, near, few, width), bf16),
+        VMEM((5, 4, few, width), bf16),
+        VMEM((order, width), bf16),
+        VMEM((4, few, width), bf16),
+        VMEM((3, 4, few, width), bf16),
+        VMEM((far - 1, 3, few, width), bf16),
+        VMEM((4, few, width), bf16),
+        *[pltpu.SemaphoreType.DMA((count,)) for count in PROLOGUE_COUNTS for _ in range(2)],
+    ]
+
+
+def level_shapes(level, order, left):
     near, far = near_far(level)
     span = near // LINE
     rows = order // near
-    left = width - (level - 1) * order
     shapes = [VMEM((order, left), jnp.bfloat16)]
     for size in (order, left - order):
         shapes.append(VMEM((span - 1, rows, size), jnp.bfloat16))
@@ -406,13 +447,17 @@
         return copies
 
 
-def tree_kernel(levels, first_ref, bases_ref, rights_ref, inv_ref, targets_ref, log_ref, answer_out, totals_out, *refs):
+def tree_kernel(levels, points_ref, targets_ref, noise_ref, index_ref, scales_ref, answer_out, totals_out, *refs):
     solved, answer, basis_coef, target_coef, part, base_t, rest, guess, cap, spread, logs = refs[:11]
     last = refs[11:19]
-    level_refs, at = {}, 19
-    order, width = part.shape
-    for level in range(3, levels + 1):
-        count = len(level_shapes(level, order, width))
+    root_own, root_landed, root_send, root_recv = refs[19:23]
+    rights_ref, inv_ref, first_ref, bases_ref, log_ref = refs[23:28]
+    begin, at = refs[28:55], 55
+    level_refs = {}
+    order = part.shape[0]
+    width = levels * order + LANES
+    for level in range(3, levels):
+        count = len(level_shapes(level, order, 2 * order))
         level_refs[level] = refs[at : at + count]
         at += count
     leaf = inv_ref.shape[1]
@@ -421,6 +466,9 @@
     device = lax.axis_index("narrow") * lax.axis_size("wide") + lax.axis_index("wide")
     spot = lax.rem(device, LINE)
     hail(near, far)
+    prologue(
+        points_ref, targets_ref, noise_ref, index_ref, scales_ref, rights_ref, inv_ref, first_ref, bases_ref, log_ref, begin
+    )
 
     def columns(c):
         return pl.ds(pl.multiple_of(c * order, order), order)
@@ -453,7 +501,7 @@
     def products(base, rows, level):
         high, low = halves(base.T)
         base_t[:, : base.shape[0]] = high
-        part[:, tail:] = three_dot((high, low), halves(answer[rows])).astype(jnp.bfloat16)
+        part[:, tail:width] = three_dot((high, low), halves(answer[rows])).astype(jnp.bfloat16)
 
         def chunk(c, carry):
             left = base_t[:, : base.shape[0]]
@@ -464,7 +512,7 @@
 
     def solve(level, sums, first, target):
         high, low = halves(guess[...])
-        right = sums[:, target:]
+        right = sums[:, target : target + LANES]
         target_coef[...] = one_dot(high, right) + one_dot(low, right)
 
         def chunk(c, carry):
@@ -510,7 +558,8 @@
     invert(2, inner)
     solve(2, part, 2 * order, tail)
 
-    for level in range(3, levels + 1):
+    root = levels * order - order
+    for level in range(3, levels):
         sums = LevelSum(level, part, level_refs[level])
         base_high, base_low = halves(bases_ref[:, (level - 2) * order : (level - 1) * order].T)
         base_t[...] = base_high
@@ -521,13 +570,15 @@
             return carry
 
         update(level - 1, 0)
-        if level == 3:
-            all_here(near, far)
         ahead = sums.scatter(0)
         left = take_out_targets(level - 1, everything)
         answer[...] = left
-        part[:, tail:] = three_dot((base_high, base_low), halves(left)).astype(jnp.bfloat16)
+        part[:, tail:width] = three_dot((base_high, base_low), halves(left)).astype(jnp.bfloat16)
         lax.fori_loop(level, levels, update, 0)
+        if level == levels - 1:
+            base_high, base_low = halves(bases_ref[:, root - order :].T)
+            part[:, width : width + order] = one_dot(base_high, solved[:, root:]).astype(jnp.bfloat16)
+            part[:, width + order :] = three_dot((base_high, base_low), halves(left)).astype(jnp.bfloat16)
         behind = sums.scatter(1)
         if sums.far > 1:
             ahead = sums.pass_on(0, sums.add_up(0, ahead))
@@ -546,15 +597,34 @@
             copy.wait()
         solve(level, sums.sums, order, tail - (level - 1) * order)
 
+    totals = sums.sums
+    high, low = halves(guess[...])
+    across = totals[:, order : 2 * order]
+    coef = halves(one_dot(high, across) + one_dot(low, across))
+    turned = across.astype(jnp.float32).T.astype(jnp.bfloat16)
+    root_products = totals[:, 2 * order + LANES :].astype(jnp.float32)
+    root_own[:, :order] = root_products[:, :order] - (one_dot(turned, coef[0]) + one_dot(turned, coef[1]))
+    coef = halves(target_coef[...])
+    root_own[:, order:] = root_products[:, order:] - (one_dot(turned, coef[0]) + one_dot(turned, coef[1]))
+    exchange = remote(root_own, root_landed, root_send.at[0], root_recv.at[0], far_peer(far, far // 2)[1])
+    exchange.start()
     own_rows = pl.ds(pl.multiple_of(spot * leaf, leaf), leaf)
-    own_answer = take_out_targets(levels, own_rows)
-    answer_out[...] = own_answer
-
-    landed, passed, terms, own, near_send, near_recv, far_send, far_recv = last
+    answer[own_rows] = take_out_targets(levels - 1, own_rows)
+    take_out(levels - 1, own_rows, levels - 1)
+    exchange.wait()
+    inner = root_own[:, :order] + root_landed[:, :order]
+    choose_cap(inner, lax.rem(device, 2**levels) == 2 ** (levels - 1))
     row = lax.broadcasted_iota(jnp.int32, (order, order), 0)
     lane = lax.broadcasted_iota(jnp.int32, (order, order), 1)
     cap[...] = cap[...] + jnp.where(row == lane, 1.0, 0.0)
-    gauss_jordan(cap, spread, logs, None)
+    newton_start(levels, inner, rest, guess)
+    gauss_jordan(cap, spread, logs, beside=functools.partial(newton_round, rest, guess, 0, 0))
+    right = root_own[:, order:] + root_landed[:, order:]
+    target_coef[...] = three_dot(halves(guess[...]), halves(right))
+    own_answer = take_out_targets(levels, own_rows)
+    answer_out[...] = own_answer
+
+    landed, passed, terms, own, near_send, near_recv, far_send, far_recv = last
     fits = jnp.sum(targets_ref[...] * own_answer, axis=0, keepdims=True)
     line = lax.broadcasted_iota(jnp.int32, terms.shape, 0)
     terms[...] = jnp.where(line == 0, fits, jnp.where(line == 1, logs[...] + log_ref[...], 0.0))
@@ -585,19 +655,21 @@
     totals_out[...] = total
 
 
-def tree(first_base, bases, rights, inverses, targets, leaf_log, levels):
-    points, order = first_base.shape
+def tree(points, targets, noise, index, scales):
+    leaf, feature = points.shape
+    levels, order = scales.shape[0], index.shape[0] * 4 // 9
+    points_in_line = LINE * leaf
     width = levels * order + LANES
     near, far = near_far(levels)
     dma = pltpu.SemaphoreType.DMA
     terms = (8, LANES)
     scratch = [
-        VMEM((points, levels * order), jnp.bfloat16),
-        VMEM((points, LANES), jnp.float32),
+        VMEM((points_in_line, levels * order), jnp.bfloat16),
+        VMEM((points_in_line, LANES), jnp.float32),
         VMEM((order, levels * order), jnp.bfloat16),
         VMEM((order, LANES), jnp.float32),
-        VMEM((order, width), jnp.bfloat16),
-        VMEM((order, points), jnp.bfloat16),
+        VMEM((order, width + order + LANES), jnp.bfloat16),
+        VMEM((order, points_in_line), jnp.bfloat16),
         VMEM((order, order), jnp.float32),
         VMEM((order, order), jnp.float32),
         VMEM((order, order), jnp.float32),
@@ -609,35 +681,33 @@
         VMEM(terms, jnp.float32),
         *[dma((count - 1,)) for count in (near, near, far, far)],
     ]
-    for level in range(3, levels + 1):
-        scratch += level_shapes(level, order, width)
+    scratch += [VMEM((order, order + LANES), jnp.float32)] * 2 + [dma((1,))] * 2
+    scratch += [
+        VMEM((LINE, leaf, LANES), jnp.float32),
+        VMEM((LINE, order, order), jnp.float32),
+        VMEM((points_in_line, order), jnp.float32),
+        VMEM((points_in_line, (levels - 1) * order), jnp.float32),
+        VMEM((1, LANES), jnp.float32),
+        *prologue_shapes(leaf, feature, order),
+    ]
+    for level in range(3, levels):
+        extra = order + LANES if level == levels - 1 else 0
+        scratch += level_shapes(level, order, width - (level - 1) * order + extra)
     return pl.pallas_call(
         functools.partial(tree_kernel, levels),
-        out_shape=(jax.ShapeDtypeStruct(targets.shape, jnp.float32), jax.ShapeDtypeStruct(terms, jnp.float32)),
-        in_specs=[pl.BlockSpec(memory_space=VMEM)] * 6,
+        out_shape=(jax.ShapeDtypeStruct((leaf, LANES), jnp.float32), jax.ShapeDtypeStruct(terms, jnp.float32)),
+        in_specs=[*[pl.BlockSpec(memory_space=VMEM)] * 4, pl.BlockSpec(memory_space=pltpu.SMEM)],
         out_specs=(pl.BlockSpec(memory_space=VMEM),) * 2,
         scratch_shapes=scratch,
         compiler_params=pltpu.CompilerParams(
             collective_id=2, has_side_effects=True, vmem_limit_bytes=56 * 2**20
         ),
         name="tree",
-    )(first_base, bases, rights, inverses, targets, leaf_log)
-
-
-def kern(left, right):
-    left_sq = jnp.sum(jnp.square(left.astype(jnp.float32)), axis=-1)
-    right_sq = jnp.sum(jnp.square(right.astype(jnp.float32)), axis=-1)
-    cross = jnp.einsum("...iw,...jw->...ij", left, right, preferred_element_type=jnp.float32)
-    return jnp.exp(-(left_sq[..., :, None] + right_sq[..., None, :] - 2.0 * cross) / left.shape[-1])
-
-
-def pick(points, index):
-    chosen = (index[:, None] == jnp.arange(points.shape[0], dtype=jnp.int32)[None, :]).astype(jnp.bfloat16)
-    return jnp.dot(chosen, points, preferred_element_type=jnp.float32).astype(jnp.bfloat16)
+    )(points, targets, noise, index, scales)
 
 
 def per_device(embeddings, noise, targets, level_scale, skeleton):
-    leaf, width = embeddings.shape
+    leaf, _ = embeddings.shape
     levels, _, rank = skeleton.shape
     rhs = targets.shape[1]
     wide_size = lax.axis_size("wide")
@@ -645,28 +715,15 @@
     spot = lax.rem(device, LINE)
     quarter = rank // LINE
     scales = jnp.sqrt(level_scale / rank)
-
-    gram = kern(embeddings, embeddings) + jnp.diag(noise)
     local = skeleton[:, 0, :] - (device - spot) * leaf
-    padded = jnp.pad(targets, ((0, 0), (0, LANES - rhs))).at[:, rhs].set(local[0].astype(jnp.float32))
+    padded = jnp.concatenate(
+        [targets, local[0].astype(jnp.float32)[:, None], jnp.zeros((leaf, LANES - rhs - 1), jnp.float32)], axis=1
+    )
     own_rows = lax.dynamic_slice(local[2:], (0, spot * quarter), (levels - 2, quarter))
-    blocks, rights, third_centers, upper_centers, inverses, leaf_log = prologue(
-        embeddings, padded, gram, own_rows.reshape(-1, 1)
-    )
-    points = blocks.reshape(LINE * leaf, width)
-    pair_index = rights[::2, :, rhs].astype(jnp.int32)
-    low = pick(points, jnp.concatenate([pair_index.reshape(-1), local[1]]))
-    shared_centers = jnp.concatenate(
-        [low[2 * rank :], third_centers.reshape(rank, width), upper_centers.reshape((levels - 3) * rank, width)]
-    )
-    first_base = kern(blocks.reshape(2, 2 * leaf, width), low[: 2 * rank].reshape(2, rank, width)) * scales[0]
-    bases = kern(points, shared_centers) * jnp.repeat(scales[1:], rank)[None, :]
-    answer, totals = tree(
-        first_base.reshape(LINE * leaf, rank), bases, rights, inverses, padded, leaf_log, levels
-    )
-    answer = answer[:, :rhs]
+    index = jnp.concatenate([local[1], own_rows.reshape(-1)])[:, None]
+    answer, totals = tree(embeddings, padded, noise[None, :], index, scales)
     npoints = leaf * lax.axis_size("narrow") * wide_size
-    return (answer, totals[0, :rhs] / npoints, totals[1, 0] / npoints)
+    return (answer[:, :rhs], totals[0, :rhs] / npoints, totals[1, 0] / npoints)
 
 
 def solution(mesh):

time: 217 us -> 187 us (0.86)
  Pallas kernels: 189 us -> 176 us
  matrix products: 10.7 us -> 0 us
  other arithmetic: 8.22 us -> 2.49 us
    pallas_call x1 -> x0, Pallas kernels: 41.3 us -> none  [prologue(): pl.pallas_call(prologue_kernel, out_shape=(jax.ShapeDtypeStruct((LINE, le...]
    pallas_call x1, Pallas kernels: 148 us -> 176 us  [tree(): pl.pallas_call(functools.partial(tree_kernel, levels), out_shape=(jax.Sha...]
    dot_general x4 -> x0, matrix products: 10.7 us -> none  [the longest x3 8.99 us: kern(): jnp.einsum('...iw,...jw->...ij', left, right, preferred_element_type=jnp....]
    reduce_sum x4 -> x0, other arithmetic: 3.81 us -> none  [the longest x2 2.32 us: kern(): left_sq = jnp.sum(jnp.square(left.astype(jnp.float32)), axis=-1)]
where the time goes in v1:
time: 187 us
  Pallas kernels  176 us (94%)
  local copies, waits for them, and re-layouts  5.47 us (3%)
  other arithmetic  2.49 us (1%)
  between operations  2.49 us (1%)
    pallas_call x1, Pallas kernels, tree(): pl.pallas_call(functools.partial(tree_kernel, levels), out_shape=(jax.Sha...  176 us

profile of v1, /device:TPU:1, one launch (start us, length us, event | category | flops | bytes accessed | tf_op | source)
XLA Modules:
  0.0 186.9 jit_solution(11452800231877036555)
XLA Ops:
  0.6 0.0 copy-start.1
  0.7 0.0 copy-start.2
  0.7 0.6 copy-done.2
  1.3 0.5 multiply_sqrt_fusion.scales_ref
  1.8 0.1 pad.4.clone
  1.9 0.0 copy-done.1
  1.9 0.1 dynamic-slice_reduce_fusion
  2.0 0.1 reshape.34
  2.1 0.0 copy-start
  2.1 0.1 copy.11
  2.3 0.7 copy-done
  3.0 0.1 copy.10
  3.1 0.8 maximum_maximum_fusion.targets_ref
  3.8 0.8 broadcast_in_dim.13.index_ref
  4.7 176.5 %tree.1 = (f32[256,128]{1,0:T(8,128)}, f32[8,128]{1,0:T(8,128)}) custom-call(bf16[256,256]{1,0:T(8,128)(2,1)} %points_ref.1, f32[256,128]{1,0:T(8,128)} %maximum_maximum_fusion.targets_ref, f32[1,256]{1,0:T(1,128)} %bitcast.10, s32[576,1]{1,0:T(8,128)} %broadcast_in_dim.13.index_ref, f32[7]{0:T(128)} %multiply_sqrt_fusion.scales_ref), custom_call_target="tpu_custom_call" | custom-call | tf_op jit(solution)/shard_map/tree/pallas_call | solution.py:696
  181.2 1.2 slice.26
  183.0 1.6 copy.13
  184.6 1.2 multiply_bitcast_fusion
  (5 shorter events, 0.0 us)
Async XLA Ops:
  0.6 1.3 copy-start.1
  0.7 0.7 copy-start.2
  2.1 0.8 copy-start

commit v2 on v1

--- a/solution.py
+++ b/solution.py
@@ -46,7 +46,7 @@
     return cols, logs
 
 
-def inverse128(state, spread_ref, beside):
+def inverse128(state, spread_ref, beside, middle):
     order = state.shape[0]
     lane = lax.broadcasted_iota(jnp.int32, (order, LANES), 1)
     row = lax.broadcasted_iota(jnp.int32, (order, LANES), 0)
@@ -68,16 +68,18 @@
             rest = rest - cols[j] * scaled[j : j + 1]
         if beside is not None and first % 16 == 8 and first < 96:
             beside()
+        if middle is not None and first == 72:
+            middle()
         pieces = [rest[:first], scaled, rest[last:]]
         state = jnp.concatenate([piece for piece in pieces if piece.shape[0]], axis=0)
     return state, total
 
 
-def gauss_jordan_half(matrix_ref, spread_ref, log_ref, j, beside):
+def gauss_jordan_half(matrix_ref, spread_ref, log_ref, j, beside, middle):
     half = matrix_ref.shape[0] // 2
     here = pl.ds(pl.multiple_of(j * half, half), half)
     there = pl.ds(pl.multiple_of((1 - j) * half, half), half)
-    inv, logs = inverse128(matrix_ref[here, here], spread_ref, beside)
+    inv, logs = inverse128(matrix_ref[here, here], spread_ref, beside, middle)
     log_ref[...] += logs
     scaled = exact_dot(inv, matrix_ref[here, there])
     below = matrix_ref[there, here]
@@ -87,11 +89,14 @@
     matrix_ref[here, here] = inv
 
 
-def gauss_jordan(matrix_ref, spread_ref, log_ref, between=None, beside=None):
+def gauss_jordan(matrix_ref, spread_ref, log_ref, between=None, beside=None, later=None):
     log_ref[...] = jnp.zeros_like(log_ref)
 
     def step(j, carry):
-        gauss_jordan_half(matrix_ref, spread_ref, log_ref, j, beside)
+        def middle():
+            pl.when(j == 1)(later)
+
+        gauss_jordan_half(matrix_ref, spread_ref, log_ref, j, beside, middle if later is not None else None)
         if between is not None:
             pl.when(j == 0)(between)
         return carry
@@ -265,19 +270,23 @@
         for copy in copies:
             copy.start()
 
-    gauss_jordan(inv, spread, log, between=choose)
-    total = rows[pl.ds(1, 4), column].astype(jnp.float32)
-    for k in range(1, 4):
-        copies[k - 1].wait()
-        total = total + landed[k - 1].astype(jnp.float32)
-    own[...] = total.astype(jnp.bfloat16)
-    copies = []
+    far_copies = []
     for k in range(1, far):
         device = far_peer(far, k)[1]
-        copies.append(
+        far_copies.append(
             remote(own.at[pl.ds(1, 3)], passed.at[k - 1], far_sems[0].at[k - 1], far_sems[1].at[k - 1], device)
         )
-        copies[-1].start()
+
+    def hand_on():
+        total = rows[pl.ds(1, 4), column].astype(jnp.float32)
+        for k in range(1, 4):
+            copies[k - 1].wait()
+            total = total + landed[k - 1].astype(jnp.float32)
+        own[...] = total.astype(jnp.bfloat16)
+        for copy in far_copies:
+            copy.start()
+
+    gauss_jordan(inv, spread, log, between=choose, later=hand_on)
     pair.wait()
     pair_all[line] = (rows[0].astype(jnp.float32) + pair_landed[...].astype(jnp.float32)).astype(jnp.bfloat16)
     line_copies = to_line(pair_all.at[line], pair_all.at[line], line_sems)
@@ -303,16 +312,16 @@
 
     base_everywhere(2, rows_at(points, index_ref[:order]))
     position = far_peer(far, 0)[0]
-    sums = [total[1], total[2], total[3]]
+    sums = [own[1].astype(jnp.float32), own[2].astype(jnp.float32), own[3].astype(jnp.float32)]
     for k in range(1, far):
-        copies[k - 1].wait()
+        far_copies[k - 1].wait()
         sender = lax.rem(position + far - k, far)
         core = lax.div(sender, 4) == lax.div(position, 4)
         slab = lax.div(sender, 2) == lax.div(position, 2)
         keep = [jnp.where(slab, 1.0, 0.0), jnp.where(core, 1.0, 0.0), 1.0]
         for i in range(3):
             sums[i] = sums[i] + passed[k - 1, i].astype(jnp.float32) * keep[i]
-    upper[0, block] = total[0].astype(jnp.bfloat16)
+    upper[0, block] = own[0]
     for i in range(3):
         upper[i + 1, block] = sums[i].astype(jnp.bfloat16)
     near_copies = []
@@ -447,8 +456,9 @@
         return copies
 
 
-def tree_kernel(levels, points_ref, targets_ref, noise_ref, index_ref, scales_ref, answer_out, totals_out, *refs):
+def tree_kernel(levels, points_ref, targets_ref, noise_ref, index_ref, scales_ref, answer_out, fit_out, logdet_out, *refs):
     solved, answer, basis_coef, target_coef, part, base_t, rest, guess, cap, spread, logs = refs[:11]
+    base_t_low, refs = refs[11], refs[:11] + refs[12:]
     last = refs[11:19]
     root_own, root_landed, root_send, root_recv = refs[19:23]
     rights_ref, inv_ref, first_ref, bases_ref, log_ref = refs[23:28]
@@ -510,18 +520,21 @@
 
         lax.fori_loop(level - 1, levels, chunk, 0)
 
-    def solve(level, sums, first, target):
+    def solve_chunk(level, sums, first, c):
+        right = sums[:, pl.ds(pl.multiple_of(first + (c - level) * order, LANES), order)]
+        high, low = halves(guess[...])
+        basis_coef[:, columns(c)] = (one_dot(high, right) + one_dot(low, right)).astype(jnp.bfloat16)
+
+    def solve_rest(level, sums, first, target):
         high, low = halves(guess[...])
         right = sums[:, target : target + LANES]
         target_coef[...] = one_dot(high, right) + one_dot(low, right)
 
         def chunk(c, carry):
-            right = sums[:, pl.ds(pl.multiple_of(first + (c - level) * order, LANES), order)]
-            high, low = halves(guess[...])
-            basis_coef[:, columns(c)] = (one_dot(high, right) + one_dot(low, right)).astype(jnp.bfloat16)
+            solve_chunk(level, sums, first, c)
             return carry
 
-        lax.fori_loop(level, levels, chunk, 0)
+        lax.fori_loop(level + 1, levels, chunk, 0)
 
     def take_out_targets(level, rows):
         front = solved[rows, (level - 1) * order : level * order]
@@ -541,7 +554,8 @@
         inner = part[:, :order].astype(jnp.float32)
         choose_cap(inner, (pair == lax.div(spot, 2)) & (lax.rem(device, 2) == 1))
         invert(1, inner)
-        solve(1, part, order, tail)
+        solve_chunk(1, part, order, 1)
+        solve_rest(1, part, order, tail)
         answer[rows] = take_out_targets(1, rows)
 
         def chunk(c, carry):
@@ -556,13 +570,17 @@
     inner = part[:, order : 2 * order].astype(jnp.float32)
     choose_cap(inner, lax.rem(device, 4) == 2)
     invert(2, inner)
-    solve(2, part, 2 * order, tail)
+    solve_chunk(2, part, 2 * order, 2)
+    rest_of = (2, part, 2 * order, tail)
 
     root = levels * order - order
+
+    def turn_base(level):
+        base_t[...], base_t_low[...] = halves(bases_ref[:, (level - 2) * order : (level - 1) * order].T)
+
+    turn_base(3)
     for level in range(3, levels):
         sums = LevelSum(level, part, level_refs[level])
-        base_high, base_low = halves(bases_ref[:, (level - 2) * order : (level - 1) * order].T)
-        base_t[...] = base_high
 
         def update(c, carry):
             new = take_out(level - 1, everything, c)
@@ -571,9 +589,10 @@
 
         update(level - 1, 0)
         ahead = sums.scatter(0)
+        solve_rest(*rest_of)
         left = take_out_targets(level - 1, everything)
         answer[...] = left
-        part[:, tail:width] = three_dot((base_high, base_low), halves(left)).astype(jnp.bfloat16)
+        part[:, tail:width] = three_dot((base_t[...], base_t_low[...]), halves(left)).astype(jnp.bfloat16)
         lax.fori_loop(level, levels, update, 0)
         if level == levels - 1:
             base_high, base_low = halves(bases_ref[:, root - order :].T)
@@ -588,6 +607,8 @@
         else:
             ahead = sums.gather(0, sums.add_up(0, ahead))
             behind = sums.gather(1, sums.add_up(1, behind))
+        if level < levels - 1:
+            turn_base(level + 1)
         for copy in ahead:
             copy.wait()
         inner = sums.sums[:, :order].astype(jnp.float32)
@@ -595,9 +616,13 @@
         invert(level, inner)
         for copy in behind:
             copy.wait()
-        solve(level, sums.sums, order, tail - (level - 1) * order)
+        rest_of = (level, sums.sums, order, tail - (level - 1) * order)
+        if level < levels - 1:
+            solve_chunk(level, sums.sums, order, level)
 
     totals = sums.sums
+    solve_chunk(levels - 1, totals, order, levels - 1)
+    solve_rest(*rest_of)
     high, low = halves(guess[...])
     across = totals[:, order : 2 * order]
     coef = halves(one_dot(high, across) + one_dot(low, across))
@@ -622,7 +647,7 @@
     right = root_own[:, order:] + root_landed[:, order:]
     target_coef[...] = three_dot(halves(guess[...]), halves(right))
     own_answer = take_out_targets(levels, own_rows)
-    answer_out[...] = own_answer
+    answer_out[...] = own_answer[:, : answer_out.shape[1]]
 
     landed, passed, terms, own, near_send, near_recv, far_send, far_recv = last
     fits = jnp.sum(targets_ref[...] * own_answer, axis=0, keepdims=True)
@@ -652,10 +677,12 @@
     total = passed[0]
     for k in range(1, far):
         total = total + passed[k]
-    totals_out[...] = total
-
-
-def tree(points, targets, noise, index, scales):
+    share = 1.0 / (leaf * lax.axis_size("narrow") * lax.axis_size("wide"))
+    fit_out[...] = total[0:1, : fit_out.shape[1]] * share
+    logdet_out[...] = total[1:2, 0:1] * share
+
+
+def tree(points, targets, noise, index, scales, rhs):
     leaf, feature = points.shape
     levels, order = scales.shape[0], index.shape[0] * 4 // 9
     points_in_line = LINE * leaf
@@ -675,6 +702,7 @@
         VMEM((order, order), jnp.float32),
         VMEM((8, 8, LANES), jnp.float32),
         VMEM((1, LANES), jnp.float32),
+        VMEM((order, points_in_line), jnp.bfloat16),
         VMEM((near, *terms), jnp.float32),
         VMEM((far, *terms), jnp.float32),
         VMEM(terms, jnp.float32),
@@ -695,9 +723,9 @@
         scratch += level_shapes(level, order, width - (level - 1) * order + extra)
     return pl.pallas_call(
         functools.partial(tree_kernel, levels),
-        out_shape=(jax.ShapeDtypeStruct((leaf, LANES), jnp.float32), jax.ShapeDtypeStruct(terms, jnp.float32)),
+        out_shape=tuple(jax.ShapeDtypeStruct(shape, jnp.float32) for shape in ((leaf, rhs), (1, rhs), (1, 1))),
         in_specs=[*[pl.BlockSpec(memory_space=VMEM)] * 4, pl.BlockSpec(memory_space=pltpu.SMEM)],
-        out_specs=(pl.BlockSpec(memory_space=VMEM),) * 2,
+        out_specs=(pl.BlockSpec(memory_space=VMEM),) * 3,
         scratch_shapes=scratch,
         compiler_params=pltpu.CompilerParams(
             collective_id=2, has_side_effects=True, vmem_limit_bytes=56 * 2**20
@@ -721,9 +749,8 @@
     )
     own_rows = lax.dynamic_slice(local[2:], (0, spot * quarter), (levels - 2, quarter))
     index = jnp.concatenate([local[1], own_rows.reshape(-1)])[:, None]
-    answer, totals = tree(embeddings, padded, noise[None, :], index, scales)
-    npoints = leaf * lax.axis_size("narrow") * wide_size
-    return (answer[:, :rhs], totals[0, :rhs] / npoints, totals[1, 0] / npoints)
+    answer, fit, logdet = tree(embeddings, padded, noise[None, :], index, scales, rhs)
+    return (answer, fit.reshape(rhs), logdet.reshape(()))
 
 
 def solution(mesh):

time: 187 us -> 185 us (0.989)
    unnamed x8 -> x11, local copies, waits for them, and re-layouts: 3.06 us -> 4.24 us
where the time goes in v2:
time: 185 us
  Pallas kernels  176 us (95%)
  local copies, waits for them, and re-layouts  5.47 us (3%)
  between operations  2.41 us (1%)
    pallas_call x1, Pallas kernels, tree(): pl.pallas_call(functools.partial(tree_kernel, levels), out_shape=tuple((j...  176 us
    unnamed x11, local copies, waits for them, and re-layouts  4.24 us

profile of v2, /device:TPU:1, one launch (start us, length us, event | category | flops | bytes accessed | tf_op | source)
XLA Modules:
  0.0 184.9 jit_solution(5490674093475429972)
XLA Ops:
  0.6 0.0 copy-start.1
  0.7 0.0 copy-start.2
  0.7 0.6 copy-done.2
  1.3 0.5 multiply_sqrt_fusion.scales_ref
  1.8 0.1 pad.4.clone
  1.9 0.0 copy-done.1
  1.9 0.1 dynamic-slice_reduce_fusion
  2.0 0.1 reshape.36
  2.1 0.0 copy-start
  2.1 0.1 copy.11
  2.3 0.7 copy-done
  3.0 0.1 copy.10
  3.1 0.8 maximum_maximum_fusion.targets_ref
  3.8 0.8 broadcast_in_dim.13.index_ref
  4.7 175.7 %tree.1 = (f32[256,64]{1,0:T(8,128)}, f32[1,64]{1,0:T(1,128)}, f32[1,1]{1,0:T(1,128)}) custom-call(bf16[256,256]{1,0:T(8,128)(2,1)} %points_ref.1, f32[256,128]{1,0:T(8,128)} %maximum_maximum_fusion.targets_ref, f32[1,256]{1,0:T(1,128)} %bitcast.7, s32[576,1]{1,0:T(8,128)} %broadcast_in_dim.13.index_ref, f32[7]{0:T(128)} %multiply_sqrt_fusion.scales_ref), custom_call_target="tpu_custom_call" | custom-call | tf_op jit(solution)/shard_map/tree/pallas_call | solution.py:724
  180.4 1.6 copy.13
  182.0 0.0 copy-start.3
  182.0 0.7 copy-done.3
  182.7 0.5 copy.16
  (5 shorter events, 0.0 us)
Async XLA Ops:
  0.6 1.3 copy-start.1
  0.7 0.7 copy-start.2
  2.1 0.8 copy-start
  182.0 0.7 copy-start.3
